TPU v7x, 32 devices: a whole 2x2x4 slice. The times are simulated.
32 devices in a mesh: dp: 1, sp: 32 (over x, y, z, core).
Axes of the slice: x: 2, y: 2, z: 4, core: 2. Of those that a mesh axis runs over, the one named last changes fastest.
Arguments:
- q: bfloat16 [32, 32, 96], P('dp')
- k: bfloat16 [32, 8192, 32, 96], P('dp', 'sp')
- v: bfloat16 [32, 8192, 32, 96], P('dp', 'sp')
Outputs:
- q: bfloat16 [32, 32, 96], P('dp')
All inputs are finite; a program needn't handle non-finite values.
Results may differ from a plain program's by a relative error of at most 0.012.
Values are sent between devices in bfloat16 or wider.
A program may use at most 2 GiB of HBM per device.

v0:
```python
import jax
import jax.numpy as jnp
from jax import lax
from jax.sharding import PartitionSpec as P


def einsum(form, a, b):
    return jnp.einsum(form, a.astype(jnp.float32), b.astype(jnp.float32))


def part_of(q, k, v):
    grouped = q.reshape(q.shape[0], k.shape[2], -1, q.shape[2])
    scores = einsum("bgsd,bugd->bgsu", grouped, k) * q.shape[2] ** -0.5
    high = jnp.max(scores, -1, keepdims=True)
    weights = jnp.exp(scores - high)
    seen = einsum("bgsu,bugd->bgsd", weights.astype(jnp.bfloat16), v)
    return jnp.concatenate([seen, jnp.sum(weights, -1, keepdims=True), high], -1)


def together(parts):
    seen, total, high = parts[..., :-2], parts[..., -2:-1], parts[..., -1:]
    scale = jnp.exp(high - jnp.max(high, 0))
    return (jnp.sum(seen * scale, 0) / jnp.sum(total * scale, 0)).astype(jnp.bfloat16)


def solution(mesh):
    def step(q, k, v):
        return together(lax.all_gather(part_of(q, k, v), "sp")).reshape(q.shape)

    return jax.shard_map(
        step,
        mesh=mesh,
        in_specs=(P("dp", None, None), P("dp", "sp", None, None), P("dp", "sp", None, None)),
        out_specs=P("dp", None, None),
        check_vma=False,
    )
```

profile of v0, /device:TPU:0, one launch (start us, length us, event | category | flops | bytes accessed | tf_op | source)
XLA Modules:
  0.0 225.3 jit_solution(12273565469964858757)
XLA Ops:
  6.5 0.0 all-gather.3.cloned.1.call-start
  6.5 18.0 %fusion.8 = f32[32,32,1,256]{3,2,1,0:T(1,128)S(1)} fusion(bf16[32,256,32,96]{1,3,2,0:T(8,128)(2,1)} %param.4, bf16[32,32,96,1]{2,1,0,3:T(8,128)(2,1)} %bitcast.27), kind=kOutput, calls=%fused_computation.14 | convolution fusion | flops 50331648 | bytes 51576832 | tf_op jit(solution)/shard_map/bgsd,bugd->bgsu/dot_general | solution.py:8
  24.5 0.2 fusion.5
  24.8 0.4 fusion.6
  25.2 0.3 copy.17
  25.5 0.3 copy.16
  25.8 19.7 %fusion.1 = f32[32,32,1,96]{3,2,1,0:T(1,128)S(1)} fusion(bf16[32,256,32,96]{1,3,2,0:T(8,128)(2,1)} %param.5, bf16[32,32,256,1]{2,1,0,3:T(8,128)(2,1)S(1)} %get-tuple-element.7), kind=kOutput, calls=%fused_computation.4 | convolution fusion | flops 50331648 | bytes 51249152 | tf_op jit(solution)/shard_map/bgsu,bugd->bgsd/dot_general | solution.py:8
  45.4 1.1 pad_maximum_fusion
  46.6 0.0 all-gather.3.cloned.1.call-update
  46.6 117.1 %all-gather.3.cloned.1.call-done = f32[1024,32,1,98]{3,1,2,0:T(8,128)} async-done(((f32[32,32,1,98]{3,1,2,0:T(8,128)}), f32[1024,32,1,98]{3,1,2,0:T(8,128)}) %all-gather.3.cloned.1.call-update) | async-done | bytes 12845072 | tf_op jit(solution)/shard_map/all_gather | solution.py:28
  163.7 32.3 %copy.18 = f32[1024,32,1,98]{1,0,3,2:T(8,128)} copy(f32[1024,32,1,98]{3,1,2,0:T(8,128)} %all-gather.3.cloned.1.call-done) | data formatting | bytes 25690112 | tf_op jit(solution)/shard_map/all_gather | solution.py:28
  195.9 1.1 slice_reduce_fusion
  197.0 1.3 fusion.7
  198.4 18.4 %fusion = f32[32,32,96]{1,0,2:T(8,128)S(1)} fusion(f32[32,32,32,1,98]{2,1,0,4,3:T(8,128)} %bitcast.25, f32[32,32,32]{2,1,0:T(8,128)S(1)} %get-tuple-element.6), kind=kLoop, calls=%fused_computation.1 | loop fusion | flops 6193152 | bytes 13107200 | tf_op jit(solution)/shard_map/reduce_sum | solution.py:23
  216.8 0.2 divide_convert_fusion
  217.0 1.5 copy.19
Async XLA Ops:
  6.5 157.1 %all-gather.3.cloned.1.call-start = ((), (), s32[]{:S(2)}) async-start(), calls=%async_computation | async-start | bytes 17301504 | tf_op jit(solution)/shard_map/all_gather | solution.py:28
Sparse Core Ops, SparseCore 0:
  46.7 116.9 all-gather.2
where the time goes:
time: 226 us; the launch traced here: 225 us
  waiting for transfers between devices  117 us (52%)
  matrix products  37.7 us (17%)
  local copies, waits for them, and re-layouts  34.3 us (15%)
  other arithmetic  22.8 us (10%)
  between operations  13.4 us (6%)
    all_gather x1, waiting for transfers between devices, step(): return together(lax.all_gather(part_of(q, k, v), 'sp')).reshape(q.shape)  117 us
    dot_general x2, matrix products, einsum(): return jnp.einsum(form, a.astype(jnp.float32), b.astype(jnp.float32))  37.7 us
    all_gather x1, local copies, waits for them, and re-layouts, step(): return together(lax.all_gather(part_of(q, k, v), 'sp')).reshape(q.shape)  32.3 us
    reduce_sum x1, other arithmetic, together(): jnp.sum(seen * scale, 0) / jnp.sum(total * scale, 0)  18.4 us
  transfers between devices with their start and end apart: 1, of which 1 were waited for; matrix products, arithmetic and copies ran while one was open for 0% of the time, Pallas kernels for 0%

commit v1 on v0

v1 whole, which is shorter than its diff:
```python
import functools

import jax
import jax.numpy as jnp
from jax import lax
from jax.experimental import pallas as pl
from jax.experimental.pallas import tpu as pltpu
from jax.sharding import PartitionSpec as P

SLOTS = 4
HALF = 16
LANES = 128


def partner(me, step, n):
    mask, out, bit = n - 1 - step, 0, 1
    while bit < n:
        out = out + ((me // bit + mask // bit) % 2) * bit
        bit *= 2
    return out


def iotas(rows):
    shape = (rows, LANES)
    return lax.broadcasted_iota(jnp.int32, shape, 0), lax.broadcasted_iota(jnp.int32, shape, 1)


def rolled(x, shifts):
    quarter = iotas(x.shape[0])[0] % 4
    out = x
    for m in range(1, 4):
        out = jnp.where(quarter == m, pltpu.roll(x, shifts[m], 1), out)
    return out


def spread(q, head):
    row, lane = iotas(HALF)
    turned = rolled(q, (0, 96, 64, 32))
    tiles = []
    for g in range(HALF // 4):
        for t in range(3):
            at = LANES * t + lane - head * (row % 4)
            keep = (row // 4 == g) & (at >= 0) & (at < head)
            tiles.append(jnp.where(keep, turned, 0.0).astype(jnp.bfloat16))
    return jnp.concatenate(tiles, 1)


def diagonal(o):
    row, lane = iotas(8)
    m = row % 4
    out = []
    for r in range(HALF // 8):
        a, b, c = (
            jnp.where(row < 4, o[8 * r : 8 * r + 8, LANES * (6 * r + t) :][:, :LANES], o[8 * r : 8 * r + 8, LANES * (6 * r + 3 + t) :][:, :LANES])
            for t in range(3)
        )
        first = (m == 0) | ((m == 1) & (lane >= 96))
        second = (m == 1) | ((m == 2) & (lane >= 64))
        out.append(jnp.where(first, a, jnp.where(second, b, c)))
    return rolled(jnp.concatenate(out, 0), (0, 32, 64, 96))


def kernel(n, axes, q_ref, k_hbm, v_hbm, out_ref, kbuf, vbuf, qpad, parts, recv, done, ksem, vsem, send_sem, recv_sem, out_send, out_recv):
    heads, head = q_ref.shape[1], q_ref.shape[2]
    rows = HALF * head
    scale = head**-0.5
    me = lax.axis_index(axes)

    def device(i):
        return {axes: i}

    def k_copy(s):
        return pltpu.make_async_copy(k_hbm.at[partner(me, s, n)], kbuf.at[s % SLOTS], ksem.at[s % SLOTS])

    def v_copy(s):
        return pltpu.make_async_copy(v_hbm.at[partner(me, s, n)], vbuf.at[s % SLOTS], vsem.at[s % SLOTS])

    for s in range(SLOTS):
        k_copy(s).start()
        if s < SLOTS - 1:
            v_copy(s).start()

    barrier = pltpu.get_barrier_semaphore()

    def greet(s, c):
        pl.semaphore_signal(barrier, inc=1, device_id=device(partner(me, s, n)), device_id_type=pl.DeviceIdType.MESH)
        return c

    lax.fori_loop(0, n - 1, greet, 0)
    qpad[...] = jnp.zeros_like(qpad)

    def scores(s):
        qpad[:, :head] = q_ref[partner(me, s, n)].astype(jnp.float32)
        out = []
        for i in range(heads // HALF):
            qd = spread(qpad[HALF * i : HALF * (i + 1)], head)
            out.append(jnp.dot(qd, kbuf[s % SLOTS, rows * i : rows * (i + 1)], preferred_element_type=jnp.float32))
        x = jnp.concatenate(out, 0) * scale
        high = jnp.max(x, -1, keepdims=True)
        w = jnp.exp(x - high)
        return w.astype(jnp.bfloat16), jnp.sum(w, -1, keepdims=True), high

    def part(s, w, total, high):
        seen = []
        for i in range(heads // HALF):
            o = lax.dot_general(
                w[HALF * i : HALF * (i + 1)],
                vbuf[s % SLOTS, rows * i : rows * (i + 1)],
                (((1,), (1,)), ((), ())),
                preferred_element_type=jnp.float32,
            )
            seen.append(diagonal(o))
        lane = iotas(heads)[1]
        return jnp.where(lane < head, jnp.concatenate(seen, 0), jnp.where(lane == head, total, high))

    def part_copy(s):
        to = partner(me, s, n)
        return pltpu.make_async_remote_copy(
            src_ref=parts.at[s],
            dst_ref=recv.at[s],
            send_sem=send_sem.at[s],
            recv_sem=recv_sem.at[s],
            device_id=device(to),
            device_id_type=pl.DeviceIdType.MESH,
        )

    def out_copy(s):
        to = partner(me, s, n)
        return pltpu.make_async_remote_copy(
            src_ref=done,
            dst_ref=out_ref.at[me],
            send_sem=out_send.at[s],
            recv_sem=out_recv.at[s],
            device_id=device(to),
            device_id_type=pl.DeviceIdType.MESH,
        )

    k_copy(0).wait()
    first = scores(0)
    pl.semaphore_wait(barrier, n - 1)

    def body(s, carry):
        @pl.when((s >= 1) & (s + SLOTS - 1 < n))
        def _():
            k_copy(s + SLOTS - 1).start()

        @pl.when(s + SLOTS - 1 < n)
        def _():
            v_copy(s + SLOTS - 1).start()

        v_copy(s).wait()
        k_copy(s + 1).wait()
        parts[s] = part(s, *carry)
        after = scores(s + 1)
        part_copy(s).start()
        return after

    last = lax.fori_loop(0, n - 1, body, first)
    v_copy(n - 1).wait()
    recv[n - 1] = part(n - 1, *last)

    def arrived(s, c):
        part_copy(s).wait_recv()
        return c

    lax.fori_loop(0, n - 1, arrived, 0)
    lane = iotas(heads)[1]

    def highest(s, top):
        return jnp.maximum(top, recv[s])

    top = recv[0]
    for s in range(1, n):
        top = jnp.maximum(top, recv[s])
    top = top[:, head + 1 : head + 2]
    acc = jnp.zeros((heads, LANES), jnp.float32)
    for s in range(n):
        x = recv[s]
        acc = acc + x * jnp.exp(x[:, head + 1 : head + 2] - top)
    result = (acc / acc[:, head : head + 1])[:, :head].astype(jnp.bfloat16)
    done[...] = result
    out_ref[me] = result

    def tell(s, c):
        out_copy(s).start()
        return c

    lax.fori_loop(0, n - 1, tell, 0)

    def finish(s, c):
        part_copy(s).wait_send()
        out_copy(s).wait()
        return c

    lax.fori_loop(0, n - 1, finish, 0)


def solution(mesh):
    n = mesh.shape["sp"]

    def step(q, k, v):
        batch, tokens, heads, head = k.shape
        k, v = (x.transpose(0, 2, 3, 1).reshape(batch, heads * head, tokens) for x in (k, v))
        dma = pltpu.SemaphoreType.DMA
        return pl.pallas_call(
            functools.partial(kernel, n, "sp"),
            out_shape=jax.ShapeDtypeStruct(q.shape, jnp.bfloat16),
            in_specs=[pl.BlockSpec(memory_space=pltpu.VMEM), pl.BlockSpec(memory_space=pl.ANY), pl.BlockSpec(memory_space=pl.ANY)],
            out_specs=pl.BlockSpec(memory_space=pltpu.VMEM),
            scratch_shapes=[
                pltpu.VMEM((SLOTS, heads * head, tokens), jnp.bfloat16),
                pltpu.VMEM((SLOTS, heads * head, tokens), jnp.bfloat16),
                pltpu.VMEM((heads, LANES), jnp.float32),
                pltpu.VMEM((n, heads, LANES), jnp.float32),
                pltpu.VMEM((n, heads, LANES), jnp.float32),
                pltpu.VMEM((heads, head), jnp.bfloat16),
                dma((SLOTS,)),
                dma((SLOTS,)),
                dma((n,)),
                dma((n,)),
                dma((n,)),
                dma((n,)),
            ],
            compiler_params=pltpu.CompilerParams(collective_id=0, has_side_effects=True, vmem_limit_bytes=60 * 2**20),
        )(q, k, v)

    return jax.shard_map(
        step,
        mesh=mesh,
        in_specs=(P("dp", None, None), P("dp", "sp", None, None), P("dp", "sp", None, None)),
        out_specs=P("dp", None, None),
        check_vma=False,
    )
```

time: 226 us -> 49.1 us (0.22)
  waiting for transfers between devices: 117 us -> 0 us
  Pallas kernels: 0 us -> 47.3 us
  matrix products: 37.7 us -> 0 us
  local copies, waits for them, and re-layouts: 34.3 us -> 1.67 us
  other arithmetic: 22.8 us -> 0 us
  between operations: 13.4 us -> 0.01 us
    all_gather x1 -> x0, waiting for transfers between devices: 117 us -> none  [step(): return together(lax.all_gather(part_of(q, k, v), 'sp')).reshape(q.shape)]
    pallas_call x0 -> x1, Pallas kernels: none -> 47.3 us  [step(): pl.pallas_call(functools.partial(kernel, n, 'sp'), out_shape=jax.ShapeDty...]
    dot_general x2 -> x0, matrix products: 37.7 us -> none  [einsum(): return jnp.einsum(form, a.astype(jnp.float32), b.astype(jnp.float32))]
    all_gather x1 -> x0, local copies, waits for them, and re-layouts: 32.3 us -> none  [step(): return together(lax.all_gather(part_of(q, k, v), 'sp')).reshape(q.shape)]
    reduce_sum x2 -> x0, other arithmetic: 19.7 us -> none  [the longest x1 18.4 us: together(): jnp.sum(seen * scale, 0) / jnp.sum(total * scale, 0)]
  transfers between devices with their start and end apart: 1 -> 0, of which waited for: 1 -> 0; matrix products, arithmetic and copies ran while one was open for 0% -> 0% of each run, Pallas kernels for 0% -> 0%
where the time goes in v1:
time: 49.1 us; the launch traced here: 48.9 us
  Pallas kernels  47.3 us (96%)
  local copies, waits for them, and re-layouts  1.67 us (3%)
    pallas_call x1, Pallas kernels, step(): pl.pallas_call(functools.partial(kernel, n, 'sp'), out_shape=jax.ShapeDty...  47.3 us
    unnamed x1, local copies, waits for them, and re-layouts  1.67 us

profile of v1, /device:TPU:0, one launch (start us, length us, event | category | flops | bytes accessed | tf_op | source)
XLA Modules:
  0.0 48.9 jit_solution(12349844567069457214)
XLA Ops:
  0.0 47.3 %shard_map.37 = bf16[32,32,96]{2,1,0:T(8,128)(2,1)} custom-call(bf16[32,32,96]{2,1,0:T(8,128)(2,1)} %q_ref.1, bf16[32,3072,256]{2,1,0:T(8,128)(2,1)} %bitcast.6, bf16[32,3072,256]{2,1,0:T(8,128)(2,1)} %bitcast.7), custom_call_target="tpu_custom_call" | custom-call | tf_op jit(solution)/shard_map/pallas_call | solution.py:205
  47.3 1.7 %copy.5 = bf16[32,32,96]{2,1,0:T(8,128)(2,1)} copy(bf16[32,32,96]{2,1,0:T(8,128)(2,1)} %shard_map.37) | data formatting | bytes 393216

commit v2 on v1

v2 whole, which is shorter than its diff:
```python
import functools

import jax
import jax.numpy as jnp
from jax import lax
from jax.experimental import pallas as pl
from jax.experimental.pallas import tpu as pltpu
from jax.sharding import PartitionSpec as P


TURN = 4
HALF = 16
LANES = 128
MESH = pl.DeviceIdType.MESH


def iotas(rows):
    shape = (rows, LANES)
    return lax.broadcasted_iota(jnp.int32, shape, 0), lax.broadcasted_iota(jnp.int32, shape, 1)


def rolled(x, shifts):
    quarter = iotas(x.shape[0])[0] % 4
    out = x
    for m in range(1, 4):
        out = jnp.where(quarter == m, pltpu.roll(x, shifts[m], 1), out)
    return out


def spread(q, head):
    row, lane = iotas(HALF)
    turned = rolled(q, (0, 96, 64, 32))
    tiles = []
    for g in range(HALF // 4):
        for t in range(3):
            at = LANES * t + lane - head * (row % 4)
            keep = (row // 4 == g) & (at >= 0) & (at < head)
            tiles.append(jnp.where(keep, turned, 0.0).astype(jnp.bfloat16))
    return jnp.concatenate(tiles, 1)


def diagonal(o):
    row, lane = iotas(8)
    m = row % 4
    out = []
    for r in range(HALF // 8):
        a, b, c = (
            jnp.where(row < 4, o[8 * r : 8 * r + 8, LANES * (6 * r + t) :][:, :LANES], o[8 * r : 8 * r + 8, LANES * (6 * r + 3 + t) :][:, :LANES])
            for t in range(3)
        )
        first = (m == 0) | ((m == 1) & (lane >= 96))
        second = (m == 1) | ((m == 2) & (lane >= 64))
        out.append(jnp.where(first, a, jnp.where(second, b, c)))
    return rolled(jnp.concatenate(out, 0), (0, 32, 64, 96))


def kernel(n, axis, q_hbm, k_hbm, v_hbm, out_ref, kbuf, vbuf, qbuf, qpad, parts, recv, done, qsem, ksem, vsem, send_sem, recv_sem, out_send, out_recv):
    heads, head = q_hbm.shape[1], q_hbm.shape[2]
    rows = HALF * head
    scale = head**-0.5
    turns = n // TURN
    me = lax.axis_index(axis)
    bits = n.bit_length() - 1
    low = TURN.bit_length() - 1
    flips = [2**i - 2 ** (i + 1) * lax.rem(lax.div(me, 2**i), 2) for i in range(bits)]

    def peer(mask):
        out = me
        for i in range(bits):
            if mask >> i & 1:
                out = out + flips[i]
        return out

    lows = [peer(TURN - 1 - u) for u in range(TURN)]

    def owner(turn, u):
        if isinstance(turn, int):
            return peer(n - 1 - TURN * turn - u)
        out, mask = lows[u], turns - 1 - turn
        for i in range(low, bits):
            out = out + lax.rem(lax.div(mask, 2 ** (i - low)), 2) * flips[i]
        return out

    def at(turn, u):
        return turn + u // TURN, u % TURN

    def k_copy(turn, u):
        turn, u = at(turn, u)
        return pltpu.make_async_copy(k_hbm.at[owner(turn, u)], kbuf.at[u], ksem.at[u])

    def v_copy(turn, u):
        turn, u = at(turn, u)
        return pltpu.make_async_copy(v_hbm.at[owner(turn, u)], vbuf.at[u], vsem.at[u])

    q_copy = pltpu.make_async_copy(q_hbm, qbuf, qsem)
    k_copy(0, 0).start()
    q_copy.start()
    k_copy(0, 1).start()
    for u in range(TURN):
        v_copy(0, u).start()
        if u + 2 < TURN:
            k_copy(0, u + 2).start()

    barrier = pltpu.get_barrier_semaphore()
    for mask in range(n - 1, 0, -1):
        pl.semaphore_signal(barrier, inc=1, device_id={axis: peer(mask)}, device_id_type=MESH)
    qpad[...] = jnp.zeros_like(qpad)

    def scores(turn, u):
        turn, u = at(turn, u)
        qpad[u, :, :head] = qbuf[owner(turn, u)].astype(jnp.float32)
        out = []
        for i in range(heads // HALF):
            qd = spread(qpad[u, HALF * i : HALF * (i + 1)], head)
            out.append(jnp.dot(qd, kbuf[u, rows * i : rows * (i + 1)], preferred_element_type=jnp.float32))
        return jnp.concatenate(out, 0)

    def weigh(x):
        x = x * scale
        high = jnp.max(x, -1, keepdims=True)
        w = jnp.exp(x - high)
        return w.astype(jnp.bfloat16), jnp.sum(w, -1, keepdims=True), high

    def part(u, w, total, high):
        seen = []
        for i in range(heads // HALF):
            o = lax.dot_general(
                w[HALF * i : HALF * (i + 1)],
                vbuf[u, rows * i : rows * (i + 1)],
                (((1,), (1,)), ((), ())),
                preferred_element_type=jnp.float32,
            )
            seen.append(diagonal(o))
        lane = iotas(heads)[1]
        return jnp.where(lane < head, jnp.concatenate(seen, 0), jnp.where(lane == head, total, high))

    def part_copy(s, to):
        return pltpu.make_async_remote_copy(
            src_ref=parts.at[s], dst_ref=recv.at[s], send_sem=send_sem.at[s], recv_sem=recv_sem.at[s], device_id={axis: to}, device_id_type=MESH
        )

    def out_copy(mask, to=None):
        held = out_ref.at[me if to is None else peer(mask ^ to)]
        return pltpu.make_async_remote_copy(
            src_ref=done if to is None else held,
            dst_ref=held,
            send_sem=out_send.at[mask],
            recv_sem=out_recv.at[mask],
            device_id={axis: peer(mask if to is None else to)},
            device_id_type=MESH,
        )

    q_copy.wait()
    k_copy(0, 0).wait()
    x0 = scores(0, 0)
    k_copy(1, 0).start()
    k_copy(0, 1).wait()
    x1 = scores(0, 1)
    k_copy(1, 1).start()
    pl.semaphore_wait(barrier, n - 1)

    def steps(turn, carry, final):
        weighed, x = carry
        for u in range(TURN):
            s = TURN * turn + u
            v_copy(turn, u).wait()
            if not (final and u + 2 >= TURN):
                k_copy(turn, u + 2).wait()
            p = part(u, *weighed)
            if not (final and u + 1 >= TURN):
                weighed = weigh(x)
            if not (final and u + 2 >= TURN):
                x = scores(turn, u + 2)
            if final and u == TURN - 1:
                recv[s] = p
            else:
                parts[s] = p
                part_copy(s, owner(turn, u)).start()
            if not final:
                v_copy(turn + 1, u).start()
                if not (isinstance(turn, int) and turn == turns - 2 and u + 2 >= TURN):
                    k_copy(turn + 1, u + 2).start()
        return weighed, x

    carry = (weigh(x0), x1)
    carry = lax.fori_loop(0, turns - 2, lambda t, c: steps(t, c, False), carry)
    carry = steps(turns - 2, carry, False)
    steps(turns - 1, carry, True)

    for s in range(n - 1):
        part_copy(s, me).wait_recv()

    top = recv[0]
    for s in range(1, n):
        top = jnp.maximum(top, recv[s])
    top = top[:, head + 1 : head + 2]
    acc = jnp.zeros((heads, LANES), jnp.float32)
    for s in range(n):
        x = recv[s]
        acc = acc + x * jnp.exp(x[:, head + 1 : head + 2] - top)
    result = (acc / acc[:, head : head + 1])[:, :head].astype(jnp.bfloat16)
    done[...] = result
    out_ref[me] = result

    def hops(mask):
        return (mask >> 4 & 1) + (mask >> 3 & 1) + (mask >> 1 & 3)

    away = sorted(range(2, n, 2), key=hops, reverse=True)
    copies = [out_copy(m) for m in [1] + away]
    for c in copies:
        c.start()
    for m in reversed(away):
        out_copy(m).wait_recv()
        copies.append(out_copy(m + 1, 1))
        copies[-1].start()
    for c in copies:
        c.wait_send()
    for m in range(1, n, 2):
        out_copy(m).wait_recv()
    for s in range(n - 1):
        part_copy(s, me).wait_send()


def solution(mesh):
    n = mesh.shape["sp"]

    def step(q, k, v):
        batch, tokens, heads, head = k.shape
        k, v = (x.transpose(0, 2, 3, 1).reshape(batch, heads * head, tokens) for x in (k, v))
        dma = pltpu.SemaphoreType.DMA
        hbm = pl.BlockSpec(memory_space=pltpu.HBM)
        return pl.pallas_call(
            functools.partial(kernel, n, "sp"),
            out_shape=pltpu.VMEM(q.shape, jnp.bfloat16),
            in_specs=[hbm] * 3,
            out_specs=pl.BlockSpec(memory_space=pltpu.VMEM),
            scratch_shapes=[
                pltpu.VMEM((TURN, heads * head, tokens), jnp.bfloat16),
                pltpu.VMEM((TURN, heads * head, tokens), jnp.bfloat16),
                pltpu.VMEM(q.shape, jnp.bfloat16),
                pltpu.VMEM((TURN, heads, LANES), jnp.float32),
                pltpu.VMEM((n, heads, LANES), jnp.float32),
                pltpu.VMEM((n, heads, LANES), jnp.float32),
                pltpu.VMEM((heads, head), jnp.bfloat16),
                dma,
                dma((TURN,)),
                dma((TURN,)),
                dma((n,)),
                dma((n,)),
                dma((n,)),
                dma((n,)),
            ],
            compiler_params=pltpu.CompilerParams(collective_id=0, has_side_effects=True, vmem_limit_bytes=60 * 2**20),
        )(q, k, v)

    return jax.shard_map(
        step,
        mesh=mesh,
        in_specs=(P("dp", None, None), P("dp", "sp", None, None), P("dp", "sp", None, None)),
        out_specs=P("dp", None, None),
        check_vma=False,
    )
```

time: 49.1 us -> 45 us (0.916)
  Pallas kernels: 47.3 us -> 44.2 us
  local copies, waits for them, and re-layouts: 1.67 us -> 0.71 us
    pallas_call x1, Pallas kernels: 47.3 us -> 44.2 us  [step(): pl.pallas_call(functools.partial(kernel, n, 'sp'), out_shape=pltpu.VMEM(q...]
    unnamed x1, local copies, waits for them, and re-layouts: 1.67 us -> 0.71 us
where the time goes in v2:
time: 45 us; the launch traced here: 44.9 us
  Pallas kernels  44.2 us (98%)
  local copies, waits for them, and re-layouts  0.71 us (2%)
    pallas_call x1, Pallas kernels, step(): pl.pallas_call(functools.partial(kernel, n, 'sp'), out_shape=pltpu.VMEM(q...  44.2 us

profile of v2, /device:TPU:0, one launch (start us, length us, event | category | flops | bytes accessed | tf_op | source)
XLA Modules:
  0.0 44.9 jit_solution(18058611204060677832)
XLA Ops:
  0.0 44.2 %shard_map.37 = bf16[32,32,96]{2,1,0:T(8,128)(2,1)S(1)} custom-call(bf16[32,32,96]{2,1,0:T(8,128)(2,1)} %q_hbm.1, bf16[32,3072,256]{2,1,0:T(8,128)(2,1)} %bitcast.6, bf16[32,3072,256]{2,1,0:T(8,128)(2,1)} %bitcast.7), custom_call_target="tpu_custom_call" | custom-call | tf_op jit(solution)/shard_map/pallas_call | solution.py:232
  44.2 0.7 %copy.5 = bf16[32,32,96]{2,1,0:T(8,128)(2,1)} copy(bf16[32,32,96]{2,1,0:T(8,128)(2,1)S(1)} %shard_map.37) | data formatting | bytes 393216

commit v3 on v2

--- a/solution.py
+++ b/solution.py
@@ -10,6 +10,9 @@
 
 TURN = 4
 HALF = 16
+PERM = (0, 3, 1, 2, 4)
+ORDER = (3, 2, 1, 0)
+EARLY = 24
 LANES = 128
 MESH = pl.DeviceIdType.MESH
 
@@ -43,7 +46,7 @@
     row, lane = iotas(8)
     m = row % 4
     out = []
-    for r in range(HALF // 8):
+    for r in range(o.shape[0] // 8):
         a, b, c = (
             jnp.where(row < 4, o[8 * r : 8 * r + 8, LANES * (6 * r + t) :][:, :LANES], o[8 * r : 8 * r + 8, LANES * (6 * r + 3 + t) :][:, :LANES])
             for t in range(3)
@@ -54,7 +57,7 @@
     return rolled(jnp.concatenate(out, 0), (0, 32, 64, 96))
 
 
-def kernel(n, axis, q_hbm, k_hbm, v_hbm, out_ref, kbuf, vbuf, qbuf, qpad, parts, recv, done, qsem, ksem, vsem, send_sem, recv_sem, out_send, out_recv):
+def kernel(n, axis, q_hbm, k_hbm, v_hbm, out_ref, kbuf, vbuf, qbuf, qpad, parts, recv, done, qsem, ksem, vsem, lastsem, send_sem, recv_sem, out_send, out_recv):
     heads, head = q_hbm.shape[1], q_hbm.shape[2]
     rows = HALF * head
     scale = head**-0.5
@@ -71,14 +74,17 @@
                 out = out + flips[i]
         return out
 
-    lows = [peer(TURN - 1 - u) for u in range(TURN)]
+    def flipped(mask):
+        return sum((mask >> i & 1) << PERM[i] for i in range(bits))
+
+    lows = [peer(flipped(ORDER[u])) for u in range(TURN)]
 
     def owner(turn, u):
         if isinstance(turn, int):
-            return peer(n - 1 - TURN * turn - u)
+            return peer(flipped(TURN * (turns - 1 - turn) + ORDER[u]))
         out, mask = lows[u], turns - 1 - turn
         for i in range(low, bits):
-            out = out + lax.rem(lax.div(mask, 2 ** (i - low)), 2) * flips[i]
+            out = out + lax.rem(lax.div(mask, 2 ** (i - low)), 2) * flips[PERM[i]]
         return out
 
     def at(turn, u):
@@ -91,6 +97,12 @@
     def v_copy(turn, u):
         turn, u = at(turn, u)
         return pltpu.make_async_copy(v_hbm.at[owner(turn, u)], vbuf.at[u], vsem.at[u])
+
+    def last_copies():
+        return [
+            pltpu.make_async_copy(v_hbm.at[me, pl.ds(rows * i, rows)], vbuf.at[TURN - 1, pl.ds(rows * i, rows)], lastsem.at[i])
+            for i in range(heads // HALF)
+        ]
 
     q_copy = pltpu.make_async_copy(q_hbm, qbuf, qsem)
     k_copy(0, 0).start()
@@ -121,32 +133,31 @@
         w = jnp.exp(x - high)
         return w.astype(jnp.bfloat16), jnp.sum(w, -1, keepdims=True), high
 
+    def seen(u, i, w):
+        return lax.dot_general(
+            w[HALF * i : HALF * (i + 1)], vbuf[u, rows * i : rows * (i + 1)], (((1,), (1,)), ((), ())), preferred_element_type=jnp.float32
+        )
+
+    def packed(o, total, high):
+        lane = iotas(heads)[1]
+        return jnp.where(lane < head, jnp.concatenate([diagonal(x) for x in o], 0), jnp.where(lane == head, total, high))
+
     def part(u, w, total, high):
-        seen = []
-        for i in range(heads // HALF):
-            o = lax.dot_general(
-                w[HALF * i : HALF * (i + 1)],
-                vbuf[u, rows * i : rows * (i + 1)],
-                (((1,), (1,)), ((), ())),
-                preferred_element_type=jnp.float32,
-            )
-            seen.append(diagonal(o))
-        lane = iotas(heads)[1]
-        return jnp.where(lane < head, jnp.concatenate(seen, 0), jnp.where(lane == head, total, high))
+        return packed([seen(u, i, w) for i in range(heads // HALF)], total, high)
 
     def part_copy(s, to):
         return pltpu.make_async_remote_copy(
             src_ref=parts.at[s], dst_ref=recv.at[s], send_sem=send_sem.at[s], recv_sem=recv_sem.at[s], device_id={axis: to}, device_id_type=MESH
         )
 
-    def out_copy(mask, to=None):
+    def out_copy(mask, to=None, device=None):
         held = out_ref.at[me if to is None else peer(mask ^ to)]
         return pltpu.make_async_remote_copy(
             src_ref=done if to is None else held,
             dst_ref=held,
             send_sem=out_send.at[mask],
             recv_sem=out_recv.at[mask],
-            device_id={axis: peer(mask if to is None else to)},
+            device_id={axis: peer(mask if to is None else to) if device is None else device},
             device_id_type=MESH,
         )
 
@@ -159,45 +170,82 @@
     k_copy(1, 1).start()
     pl.semaphore_wait(barrier, n - 1)
 
-    def steps(turn, carry, final):
+    def start_all(copies):
+        for c in copies:
+            c.start()
+
+    def steps(turn, carry):
         weighed, x = carry
         for u in range(TURN):
             s = TURN * turn + u
             v_copy(turn, u).wait()
-            if not (final and u + 2 >= TURN):
-                k_copy(turn, u + 2).wait()
+            k_copy(turn, u + 2).wait()
             p = part(u, *weighed)
-            if not (final and u + 1 >= TURN):
-                weighed = weigh(x)
-            if not (final and u + 2 >= TURN):
-                x = scores(turn, u + 2)
-            if final and u == TURN - 1:
-                recv[s] = p
+            weighed = weigh(x)
+            x = scores(turn, u + 2)
+            parts[s] = p
+            part_copy(s, owner(turn, u)).start()
+            if not isinstance(turn, int):
+                v_copy(turn + 1, u).start()
+                k_copy(turn + 1, u + 2).start()
+            elif u < 2:
+                v_copy(turn + 1, u).start()
+                if u == 1:
+                    k_copy(turn + 1, 2).start()
+            elif u == 2:
+                k_copy(turn + 1, 3).start()
+                v_copy(turn + 1, 2).start()
             else:
-                parts[s] = p
-                part_copy(s, owner(turn, u)).start()
-            if not final:
-                v_copy(turn + 1, u).start()
-                if not (isinstance(turn, int) and turn == turns - 2 and u + 2 >= TURN):
-                    k_copy(turn + 1, u + 2).start()
+                start_all(last_copies())
         return weighed, x
 
+    def gather(first, last):
+        top = recv[first]
+        for s in range(first + 1, last):
+            top = jnp.maximum(top, recv[s])
+        top = top[:, head + 1 : head + 2]
+        acc = jnp.zeros((heads, LANES), jnp.float32)
+        for s in range(first, last):
+            x = recv[s]
+            acc = acc + x * jnp.exp(x[:, head + 1 : head + 2] - top)
+        return acc, top
+
     carry = (weigh(x0), x1)
-    carry = lax.fori_loop(0, turns - 2, lambda t, c: steps(t, c, False), carry)
-    carry = steps(turns - 2, carry, False)
-    steps(turns - 1, carry, True)
-
-    for s in range(n - 1):
+    carry = lax.fori_loop(0, turns - 2, steps, carry)
+    weighed, x = steps(turns - 2, carry)
+    final = turns - 1
+    for s in range(EARLY):
         part_copy(s, me).wait_recv()
-
-    top = recv[0]
-    for s in range(1, n):
-        top = jnp.maximum(top, recv[s])
-    top = top[:, head + 1 : head + 2]
-    acc = jnp.zeros((heads, LANES), jnp.float32)
-    for s in range(n):
-        x = recv[s]
-        acc = acc + x * jnp.exp(x[:, head + 1 : head + 2] - top)
+    early, before = gather(0, EARLY)
+
+    def send(s, p):
+        parts[s] = p
+        part_copy(s, owner(final, s % TURN)).start()
+
+    v_copy(final, 0).wait()
+    p, weighed = part(0, *weighed), weigh(x)
+    send(n - 4, p)
+    v_copy(final, 1).wait()
+    send(n - 3, part(1, *weighed))
+    k_copy(final, 2).wait()
+    x = scores(final, 2)
+    k_copy(final, 3).wait()
+    weighed, x = weigh(x), scores(final, 3)
+    v_copy(final, 2).wait()
+    o = [seen(2, i, weighed[0]) for i in range(heads // HALF)]
+    own = weigh(x)
+    send(n - 2, packed(o, *weighed[1:]))
+    halves = last_copies()
+    halves[0].wait()
+    ends = [seen(3, 0, own[0])]
+    halves[1].wait()
+    ends.append(seen(3, 1, own[0]))
+    recv[n - 1] = packed(ends, *own[1:])
+    for s in range(EARLY, n - 1):
+        part_copy(s, me).wait_recv()
+    late, after = gather(EARLY, n)
+    top = jnp.maximum(before, after)
+    acc = early * jnp.exp(before - top) + late * jnp.exp(after - top)
     result = (acc / acc[:, head : head + 1])[:, :head].astype(jnp.bfloat16)
     done[...] = result
     out_ref[me] = result
@@ -207,8 +255,15 @@
 
     away = sorted(range(2, n, 2), key=hops, reverse=True)
     copies = [out_copy(m) for m in [1] + away]
-    for c in copies:
-        c.start()
+    home = me - lax.rem(me, 2)
+    copies[0].start()
+
+    @pl.when(home != 0)
+    def _():
+        out_copy(home, None, lax.rem(me, 2)).start()
+
+    for m, c in zip(away, copies[1:]):
+        pl.when(home != m)(c.start)
     for m in reversed(away):
         out_copy(m).wait_recv()
         copies.append(out_copy(m + 1, 1))
@@ -245,6 +300,7 @@
                 dma,
                 dma((TURN,)),
                 dma((TURN,)),
+                dma((heads // HALF,)),
                 dma((n,)),
                 dma((n,)),
                 dma((n,)),

time: 45 us -> 43.7 us (0.971)
  Pallas kernels: 44.2 us -> 42.9 us
    pallas_call x1, Pallas kernels: 44.2 us -> 42.9 us  [step(): pl.pallas_call(functools.partial(kernel, n, 'sp'), out_shape=pltpu.VMEM(q...]
where the time goes in v3:
time: 43.7 us; the launch traced here: 43.6 us
  Pallas kernels  42.9 us (98%)
  local copies, waits for them, and re-layouts  0.71 us (2%)
    pallas_call x1, Pallas kernels, step(): pl.pallas_call(functools.partial(kernel, n, 'sp'), out_shape=pltpu.VMEM(q...  42.9 us

profile of v3, /device:TPU:0, one launch (start us, length us, event | category | flops | bytes accessed | tf_op | source)
XLA Modules:
  0.0 43.6 jit_solution(14060865759115148856)
XLA Ops:
  0.0 42.9 %shard_map.37 = bf16[32,32,96]{2,1,0:T(8,128)(2,1)S(1)} custom-call(bf16[32,32,96]{2,1,0:T(8,128)(2,1)} %q_hbm.1, bf16[32,3072,256]{2,1,0:T(8,128)(2,1)} %bitcast.6, bf16[32,3072,256]{2,1,0:T(8,128)(2,1)} %bitcast.7), custom_call_target="tpu_custom_call" | custom-call | tf_op jit(solution)/shard_map/pallas_call | solution.py:287
  42.9 0.7 %copy.5 = bf16[32,32,96]{2,1,0:T(8,128)(2,1)} copy(bf16[32,32,96]{2,1,0:T(8,128)(2,1)S(1)} %shard_map.37) | data formatting | bytes 393216
